TPU v7x, 32 devices: a whole 2x2x4 slice. The times are simulated.
32 devices in a mesh: groups: 2 (over y), gx: 4 (over z), gy: 4 (over x, core).
Axes of the slice: x: 2, y: 2, z: 4, core: 2. Of those that a mesh axis runs over, the one named last changes fastest.
Arguments:
- hidden_in: bfloat16 [128, 18432], P(('groups', 'gx'), 'gy'), parts along dimension 0, may hold values from -6 to 6
- w_query: bfloat16 [18432, 12288], P('gy', 'gx'), may hold values from -0.046875 to 0.046875
- w_out: bfloat16 [12288, 18432], P('gx', 'gy'), may hold values from -0.4375 to 0.4375
- cache_keys: bfloat16 [128, 1024, 256], P(('groups', 'gx', 'gy')), parts along dimension 0, may hold values from -250 to 250
- cache_values: bfloat16 [128, 1024, 256], P(('groups', 'gx', 'gy')), parts along dimension 0, may hold values from -6 to 6
- lengths: int32 [128], P(('groups', 'gx', 'gy')), parts along dimension 0, may hold values from 128 to 1024
Outputs:
- layer_out: bfloat16 [128, 18432], P(('groups', 'gx'), 'gy'), parts along dimension 0
There are 2 independent parts, one for each index of `groups`. A program takes and returns all parts, laid end to end along the dimension named above; an argument that names none is the same for every part. Nothing has to cross between parts.
All inputs are finite; a program needn't handle non-finite values.
Results may differ from a plain program's by a relative error of at most 0.0097.
Values may be sent and summed in bfloat16 or wider, within the bound.
A program may use at most 128 MiB of HBM per device.

v0:
```python
import jax
import jax.numpy as jnp
from jax import lax
from jax.sharding import PartitionSpec as P


def body(hidden_in, w_query, w_out, cache_keys, cache_values, lengths):
    across = lax.axis_size("gx")
    within = lax.axis_size("gy")
    local_seqs = cache_keys.shape[0]
    slot_count = cache_keys.shape[1]
    head_dim = cache_keys.shape[2]
    partial_query = jnp.dot(
        lax.all_gather(hidden_in, "gx", axis=0, tiled=True),
        w_query,
        preferred_element_type=jnp.float32,
    )
    slice_width = partial_query.shape[1]
    summed = lax.psum(partial_query, "gy")
    grouped = summed.reshape(across, within, local_seqs, slice_width)
    own_rows = lax.dynamic_slice_in_dim(grouped, lax.axis_index("gy"), 1, 1)
    query_rows = own_rows.reshape(across * local_seqs, slice_width).astype(jnp.bfloat16)
    query = lax.all_to_all(query_rows, "gx", split_axis=0, concat_axis=1, tiled=True)
    head_count = query.shape[1] // head_dim
    query_heads = query.reshape(local_seqs, head_count, head_dim)
    scores = jnp.einsum("bhd,bld->bhl", query_heads, cache_keys, preferred_element_type=jnp.float32)
    scores = scores / jnp.sqrt(jnp.float32(head_dim))
    live_slots = jnp.arange(slot_count)[None, None, :] < lengths[:, None, None]
    scores = jnp.where(live_slots, scores, jnp.float32(-1e30))
    top_score = jnp.max(scores, axis=2, keepdims=True)
    expo = jnp.where(live_slots, jnp.exp(scores - top_score), jnp.float32(0.0))
    probs = (expo / jnp.sum(expo, axis=2, keepdims=True)).astype(jnp.bfloat16)
    mixed = jnp.einsum("bhl,bld->bhd", probs, cache_values, preferred_element_type=jnp.float32)
    attended = mixed.astype(jnp.bfloat16).reshape(local_seqs, head_count * head_dim)
    spread = lax.all_to_all(attended, "gx", split_axis=1, concat_axis=0, tiled=True)
    stacked = spread.reshape(across, local_seqs, slice_width)
    gathered = lax.all_gather(stacked, "gy", axis=1, tiled=True)
    head_rows = gathered.reshape(across * within * local_seqs, slice_width)
    partial_out = jnp.dot(head_rows, w_out, preferred_element_type=jnp.float32)
    result = lax.psum_scatter(partial_out, "gx", scatter_dimension=0, tiled=True)
    return result.astype(jnp.bfloat16)


def solution(mesh):
    placed = (
        P(("groups", "gx"), "gy"),
        P("gy", "gx"),
        P("gx", "gy"),
        P(("groups", "gx", "gy"), None, None),
        P(("groups", "gx", "gy"), None, None),
        P(("groups", "gx", "gy")),
    )
    return jax.shard_map(
        body, mesh=mesh, in_specs=placed, out_specs=P(("groups", "gx"), "gy"), check_vma=False
    )
```

profile of v0, /device:TPU:0, one launch (start us, length us, event | category | flops | bytes accessed | tf_op | source)
XLA Modules:
  0.0 136.7 jit_solution(8029580725478154781)
XLA Ops:
  6.5 0.0 copy-start
  6.5 18.6 %all_gather.6 = bf16[64,4608]{1,0:T(8,128)(2,1)S(1)} all-gather(bf16[16,4608]{1,0:T(8,128)(2,1)} %param.6), channel_id=1, replica_groups=mesh['groups'=2,'gx'=4,'gy'=4] {'gx'}, dimensions={0}, use_global_device_ids=true | all-gather | bytes 737280 | tf_op jit(solution)/shard_map/all_gather | solution.py:14
  25.1 12.6 %fusion.10 = f32[64,3072]{1,0:T(8,128)} fusion(bf16[64,4608]{1,0:T(8,128)(2,1)S(1)} %all_gather.6, bf16[4608,3072]{1,0:T(8,128)(2,1)} %param.7), kind=kOutput, calls=%fused_computation.15 | convolution fusion | flops 1811939328 | bytes 29687808 | tf_op jit(solution)/shard_map/dot_general | solution.py:13
  37.7 0.0 copy-start.2
  37.7 1.4 %reshape.46 = f32[4,4,4,3072]{3,2,1,0:T(4,128)S(1)} reshape(f32[64,3072]{1,0:T(8,128)} %fusion.10) | data formatting | bytes 1572864 | tf_op jit(solution)/shard_map/reshape | solution.py:20
  39.1 19.3 %all-reduce.1 = bf16[4,4,4,3072]{3,2,1,0:T(4,128)(2,1)S(1)} all-reduce(f32[4,4,4,3072]{3,2,1,0:T(4,128)S(1)} %reshape.46), channel_id=1, replica_groups=mesh['groups'=2,'gx'=4,'gy'=4] {'gy'}, use_global_device_ids=true, to_apply=%region_0.0 | all-reduce | flops 196608 | bytes 1179648 | tf_op jit(solution)/shard_map/psum | solution.py:19
  58.4 0.7 fusion.6
  59.1 4.8 %all-to-all-start = ((bf16[4,4,3072]{2,1,0:T(4,128)(2,1)}), bf16[4,4,3072]{2,1,0:T(4,128)(2,1)S(1)}, u32[]{:S(2)}, u32[]{:S(2)}) async-start(bf16[4,4,3072]{2,1,0:T(4,128)(2,1)} %fusion.6), calls=%async_computation | async-start | bytes 196608 | tf_op jit(solution)/shard_map/all_to_all | solution.py:23
  63.9 0.0 reduce-scatter.2.cloned.1.call-start
  63.9 0.0 copy-done.2
  63.9 0.1 iota_compare_fusion
  64.0 5.8 %all-to-all-done = bf16[4,4,3072]{2,1,0:T(4,128)(2,1)S(1)} async-done(((bf16[4,4,3072]{2,1,0:T(4,128)(2,1)}), bf16[4,4,3072]{2,1,0:T(4,128)(2,1)S(1)}, u32[]{:S(2)}, u32[]{:S(2)}) %all-to-all-start) | async-done | bytes 98336 | tf_op jit(solution)/shard_map/all_to_all | solution.py:23
  69.7 0.1 copy.12
  69.8 0.1 reshape.47
  69.8 0.0 copy-done
  69.9 0.7 fusion.4
  70.6 0.3 fusion.9
  70.9 2.1 %convolution_convert_fusion = bf16[4,48,256]{2,1,0:T(8,128)(2,1)S(1)} fusion(bf16[4,1024,256]{2,1,0:T(8,128)(2,1)} %param.10, f32[4,48]{1,0:T(4,128)S(1)} %fusion.9, f32[4,48,1024]{2,1,0:T(8,128)S(1)} %fusion.4, pred[4,1024]{1,0:T(4,128)(4,1)S(1)} %iota_compare_fusion), kind=kOutput, calls=%fused_computation.6 | convolution fusion | flops 101500096 | bytes 2986752 | tf_op jit(solution)/shard_map/bhl,bld->bhd/dot_general | solution.py:33
  73.1 0.1 copy.13
  73.1 8.2 %all_to_all.29 = bf16[4,4,3072]{2,0,1:T(4,128)(2,1)S(1)} all-to-all(bf16[4,4,3072]{2,0,1:T(4,128)(2,1)S(1)} %copy.13), channel_id=1, replica_groups=mesh['groups'=2,'gx'=4,'gy'=4] {'gx'}, dimensions={1} | all-to-all | bytes 196608 | tf_op jit(solution)/shard_map/all_to_all | solution.py:35
  81.3 0.1 copy.14
  81.4 6.1 %all_gather.7 = bf16[4,16,3072]{2,0,1:T(4,128)(2,1)S(1)} all-gather(bf16[4,4,3072]{2,0,1:T(4,128)(2,1)S(1)} %copy.14), channel_id=1, replica_groups=mesh['groups'=2,'gx'=4,'gy'=4] {'gy'}, dimensions={1}, use_global_device_ids=true | all-gather | bytes 491520 | tf_op jit(solution)/shard_map/all_gather | solution.py:37
  87.5 0.1 copy.15
  87.7 0.0 copy-start.1
  87.7 12.8 %fusion.11 = f32[64,4608]{1,0:T(8,128)} fusion(bf16[64,3072]{1,0:T(8,128)(2,1)S(1)} %bitcast.14, bf16[3072,4608]{1,0:T(8,128)(2,1)} %param.8), kind=kOutput, calls=%fused_computation.16 | convolution fusion | flops 1811939328 | bytes 29884416 | tf_op jit(solution)/shard_map/dot_general | solution.py:39
  100.4 0.0 reduce-scatter.2.cloned.1.call-update
  100.5 27.8 %reduce-scatter.2.cloned.1.call-done = f32[16,4608]{1,0:T(8,128)} async-done(((f32[64,4608]{1,0:T(8,128)}), f32[16,4608]{1,0:T(8,128)}) %reduce-scatter.2.cloned.1.call-update) | async-done | bytes 294928 | tf_op jit(solution)/shard_map/reduce_scatter | solution.py:40
  128.3 1.6 %convert_element_type.20 = bf16[16,4608]{1,0:T(8,128)(2,1)} convert(f32[16,4608]{1,0:T(8,128)} %reduce-scatter.2.cloned.1.call-done) | non-fusion elementwise | flops 73728 | bytes 442368 | tf_op jit(solution)/shard_map/convert_element_type | solution.py:41
  129.9 0.0 copy-done.1
  (1 shorter events, 0.0 us)
Async XLA Ops:
  6.5 63.3 %copy-start = (bf16[4,1024,256]{2,1,0:T(8,128)(2,1)S(1)}, bf16[4,1024,256]{2,1,0:T(8,128)(2,1)}, u32[]{:S(2)}) copy-start(bf16[4,1024,256]{2,1,0:T(8,128)(2,1)} %param.9) | copy-start | bytes 6291460
  37.7 26.2 %copy-start.2 = (s32[4]{0:T(128)S(1)}, s32[4]{0:T(128)}, u32[]{:S(2)}) copy-start(s32[4]{0:T(128)} %param.11) | copy-start | bytes 52
  59.1 10.6 %all-to-all-start = ((bf16[4,4,3072]{2,1,0:T(4,128)(2,1)}), bf16[4,4,3072]{2,1,0:T(4,128)(2,1)S(1)}, u32[]{:S(2)}, u32[]{:S(2)}) async-start(bf16[4,4,3072]{2,1,0:T(4,128)(2,1)} %fusion.6), calls=%async_computation | async-start | bytes 196608 | tf_op jit(solution)/shard_map/all_to_all | solution.py:23
  63.9 64.4 %reduce-scatter.2.cloned.1.call-start = ((), (), s32[]{:S(2)}) async-start(), calls=%async_computation.3 | async-start | bytes 1474560 | tf_op jit(solution)/shard_map/reduce_scatter | solution.py:40
  87.7 42.2 %copy-start.1 = (bf16[4,1024,256]{2,1,0:T(8,128)(2,1)S(1)}, bf16[4,1024,256]{2,1,0:T(8,128)(2,1)}, u32[]{:S(2)}) copy-start(bf16[4,1024,256]{2,1,0:T(8,128)(2,1)} %param.9) | copy-start | bytes 6291460
Sparse Core Ops, SparseCore 0:
  100.6 27.6 reduce-scatter.1
where the time goes:
time: 137 us
  blocking collectives  52.2 us (38%)
  waiting for transfers between devices  33.6 us (25%)
  matrix products  28.2 us (21%)
  between operations  13.5 us (10%)
  starting transfers between devices  4.82 us (4%)
  local copies, waits for them, and re-layouts  2.45 us (2%)
  other arithmetic  2.03 us (1%)
    reduce_scatter x1, waiting for transfers between devices, body(): lax.psum_scatter(partial_out, 'gx', scatter_dimension=0, tiled=True)  27.8 us
    psum x1, blocking collectives, body(): summed = lax.psum(partial_query, 'gy')  19.3 us
    all_gather x1, blocking collectives, body(): lax.all_gather(hidden_in, 'gx', axis=0, tiled=True)  18.6 us
    dot_general x1, matrix products, body(): partial_out = jnp.dot(head_rows, w_out, preferred_element_type=jnp.float32)  12.8 us
    dot_general x1, matrix products, body(): jnp.dot(lax.all_gather(hidden_in, 'gx', axis=0, tiled=True), w_query, pre...  12.6 us
    all_to_all x1, blocking collectives, body(): lax.all_to_all(attended, 'gx', split_axis=1, concat_axis=0, tiled=True)  8.21 us
    all_gather x1, blocking collectives, body(): gathered = lax.all_gather(stacked, 'gy', axis=1, tiled=True)  6.14 us
    all_to_all x1, waiting for transfers between devices, body(): lax.all_to_all(query_rows, 'gx', split_axis=0, concat_axis=1, tiled=True)  5.75 us
  transfers between devices with their start and end apart: 2, of which 2 were waited for; matrix products, arithmetic and copies ran while one was open for 0% of the time, Pallas kernels for 0%

commit v1 on v0

--- a/solution.py
+++ b/solution.py
@@ -1,10 +1,419 @@
+import functools
+
 import jax
 import jax.numpy as jnp
+import numpy as np
 from jax import lax
+from jax.experimental import pallas as pl
+from jax.experimental.pallas import tpu as pltpu
 from jax.sharding import PartitionSpec as P
 
-
-def body(hidden_in, w_query, w_out, cache_keys, cache_values, lengths):
+MESH = pl.DeviceIdType.MESH
+VMEM_LIMIT = 67043328
+
+
+def pieces(total, most):
+    return max(count for count in range(1, most + 1) if total % (count * 256) == 0)
+
+
+def permutation(dims, order):
+    moved = np.arange(int(np.prod(dims))).reshape(dims).transpose(order).reshape(-1)
+    return np.eye(moved.size, dtype=np.float32)[moved]
+
+
+def remote(src, dst, send, recv, device):
+    return pltpu.make_async_remote_copy(
+        src_ref=src, dst_ref=dst, send_sem=send, recv_sem=recv, device_id=device, device_id_type=MESH
+    )
+
+
+def kernel(
+    nz, seqs, heads, kparts, qparts, oparts, spots,
+    hidden_ref, wq_ref, wo_ref, keys_ref, values_ref, perm_ref, lengths_ref,
+    out_ref,
+    wq, wo, keys, values, perms, hid, pq, r1, s2, r2, qs, qr, at, gat, am, po,
+    in_sem, wq_sem, wo_sem,
+    hr_sem, hl_sem, hid_sem,
+    a_send, a_recv, b_send, b_recv,
+    q_send, q_recv, t_send, t_recv,
+    x_send, x_recv, c_send, c_recv, f_send, f_recv,
+    o_send, ol_recv, or_recv,
+):
+    z = lax.axis_index("gx")
+    j = lax.axis_index("gy")
+    x, c = j // 2, j % 2
+    xo, co = 1 - x, 1 - c
+    pair = x * 2 + co
+    across = xo * 2 + c
+    diag = xo * 2 + co
+    rows = hid.shape[1]
+    depth, slice_width = wq.shape
+    width = wo.shape[1]
+    hd = keys.shape[2]
+    slots = keys.shape[1]
+    kc, qc, oc = depth // kparts, slice_width // qparts, width // oparts
+    block = seqs * heads
+
+    hid_in = pltpu.make_async_copy(hidden_ref, hid.at[z], in_sem.at[0])
+    hid_in.start()
+    perm_in = pltpu.make_async_copy(perm_ref, perms, in_sem.at[1])
+    perm_in.start()
+    keys_in = pltpu.make_async_copy(keys_ref, keys, in_sem.at[2])
+    values_in = pltpu.make_async_copy(values_ref, values, in_sem.at[3])
+
+    def wq_in(k):
+        part = pl.ds(k * kc, kc)
+        return pltpu.make_async_copy(wq_ref.at[part], wq.at[part], wq_sem.at[k])
+
+    def wo_in(k):
+        part = pl.ds(k * (slice_width // kparts), slice_width // kparts)
+        return pltpu.make_async_copy(wo_ref.at[part], wo.at[part], wo_sem.at[k])
+
+    for k in range(kparts):
+        wq_in(k).start()
+
+    barrier = pltpu.get_barrier_semaphore()
+    for d in range(1, nz):
+        pl.semaphore_signal(barrier, inc=1, device_id={"gx": lax.rem(z + d, nz)}, device_id_type=MESH)
+    for peer in (pair, across):
+        pl.semaphore_signal(barrier, inc=1, device_id={"gy": peer}, device_id_type=MESH)
+    pl.semaphore_wait(barrier, nz + 1)
+
+    def hid_right(src, k):
+        part = hid.at[src, :, pl.ds(k * kc, kc)]
+        return remote(part, part, hr_sem.at[src, k], hid_sem.at[src, k], {"gx": lax.rem(z + 1, nz)})
+
+    def hid_left(src, k):
+        part = hid.at[src, :, pl.ds(k * kc, kc)]
+        return remote(part, part, hl_sem.at[src, k], hid_sem.at[src, k], {"gx": lax.rem(z + nz - 1, nz)})
+
+    hid_in.wait()
+    for k in range(kparts):
+        @pl.when(z < nz - 1)
+        def _():
+            hid_right(z, k).start()
+
+        @pl.when(z > 0)
+        def _():
+            hid_left(z, k).start()
+
+    perm_in.wait()
+
+    def perm(name):
+        start, size = spots[name]
+        return perms[start : start + size, :size]
+
+    def moved(name, value):
+        return jnp.dot(perm(name), value, preferred_element_type=jnp.float32).astype(jnp.bfloat16)
+
+    def stage_a(far, n):
+        there = xo if far else x
+        cols = pl.ds(n * qc, qc)
+        src = pq.at[pl.ds(pl.multiple_of((there * 2 + co) * rows, rows), rows), cols]
+        return remote(src, r1.at[1 if far else 0, :, cols], a_send.at[far, n], a_recv.at[far, n], {"gy": pair})
+
+    for t in range(1, nz):
+        for k in range(kparts):
+            @pl.when(z - t >= 0)
+            def _():
+                hid_right(z - t, k).wait_recv()
+
+                @pl.when(z < nz - 1)
+                def _():
+                    hid_right(z - t, k).start()
+
+            @pl.when(z + t < nz)
+            def _():
+                hid_left(z + t, k).wait_recv()
+
+                @pl.when(z > 0)
+                def _():
+                    hid_left(z + t, k).start()
+
+            if t == max(nz - 2, 1):
+                wq_in(k).wait()
+                wo_in(k).start()
+                if k == 0:
+                    keys_in.start()
+                    values_in.start()
+            if t == nz - 1:
+                piece = hid[:, :, k * kc : (k + 1) * kc].reshape(nz * rows, kc)
+                piece = moved("in", piece)
+                depths = slice(k * kc, (k + 1) * kc)
+
+                if k < kparts - 1:
+                    @pl.loop(0, qparts)
+                    def _(n):
+                        cols = pl.ds(pl.multiple_of(n * qc, qc), qc)
+                        part = jnp.dot(piece, wq[depths, cols], preferred_element_type=jnp.float32)
+                        if k > 0:
+                            part = part + pq[:, cols]
+                        pq[:, cols] = part
+                else:
+                    for n in range(qparts):
+                        cols = slice(n * qc, (n + 1) * qc)
+                        part = jnp.dot(piece, wq[depths, cols], preferred_element_type=jnp.float32)
+                        if k > 0:
+                            part = part + pq[:, cols]
+                        pq[:, cols] = part
+                        stage_a(1, n).start()
+                        stage_a(0, n).start()
+
+    def stage_b(n):
+        cols = pl.ds(n * qc, qc)
+        return remote(s2.at[:, cols], r2.at[:, cols], b_send.at[n], b_recv.at[n], {"gy": across})
+
+    for n in range(qparts):
+        cols = slice(n * qc, (n + 1) * qc)
+        stage_a(1, n).wait_recv()
+        far = pl.ds(pl.multiple_of(across * rows, rows), rows)
+        s2[:, cols] = pq[far, cols] + r1[1, :, cols]
+        stage_b(n).start()
+    tiles = []
+    for n in range(qparts):
+        cols = slice(n * qc, (n + 1) * qc)
+        stage_a(0, n).wait_recv()
+        stage_b(n).wait_recv()
+        near = pl.ds(pl.multiple_of(j * rows, rows), rows)
+        summed = (pq[near, cols] + r1[0, :, cols] + r2[:, cols]).astype(jnp.bfloat16)
+        tiles += [summed[:, h * hd : (h + 1) * hd] for h in range(qc // hd)]
+    query = moved("query", jnp.concatenate(tiles, axis=0))
+    qs[...] = query.reshape(nz, block, hd)
+
+    def q_copy(d):
+        return remote(
+            qs.at[lax.rem(z + d, nz)], qr.at[z], q_send.at[d], q_recv.at[d], {"gx": lax.rem(z + d, nz)}
+        )
+
+    def q_arrival(d):
+        return remote(
+            qs.at[z], qr.at[lax.rem(z - d + nz, nz)], q_send.at[d], q_recv.at[d], {"gx": lax.rem(z + d, nz)}
+        )
+
+    for d in range(1, nz):
+        q_copy(d).start()
+    qr[z] = qs[z]
+    keys_in.wait()
+    values_in.wait()
+    for d in range(1, nz):
+        q_arrival(d).wait_recv()
+
+    query = moved("heads", qr[...].reshape(nz * block, hd))
+    all_heads = nz * heads
+    mixed = []
+    for s in range(seqs):
+        own = query[s * all_heads : (s + 1) * all_heads]
+        scores = lax.dot_general(own, keys[s], (((1,), (1,)), ((), ())), preferred_element_type=jnp.float32)
+        scores = scores / np.float32(np.sqrt(hd))
+        live = lax.broadcasted_iota(jnp.int32, (all_heads, slots), 1) < lengths_ref[s]
+        scores = jnp.where(live, scores, jnp.float32(-1e30))
+        top = jnp.max(scores, axis=1, keepdims=True)
+        expo = jnp.where(live, jnp.exp(scores - top), jnp.float32(0.0))
+        probs = (expo / jnp.sum(expo, axis=1, keepdims=True)).astype(jnp.bfloat16)
+        mixed.append(jnp.dot(probs, values[s], preferred_element_type=jnp.float32).astype(jnp.bfloat16))
+    attended = moved("back", jnp.concatenate(mixed, axis=0))
+    at[...] = attended.reshape(nz, block, hd)
+
+    def t_copy(d):
+        return remote(
+            at.at[lax.rem(z + d, nz)], gat.at[z, j], t_send.at[d], t_recv.at[d], {"gx": lax.rem(z + d, nz)}
+        )
+
+    def t_arrival(d):
+        return remote(
+            at.at[z], gat.at[lax.rem(z - d + nz, nz), j], t_send.at[d], t_recv.at[d], {"gx": lax.rem(z + d, nz)}
+        )
+
+    def from_z(d):
+        return lax.rem(z - d + nz, nz)
+
+    def x_copy(d, slot):
+        part = gat.at[from_z(d), slot]
+        return remote(part, part, x_send.at[d], x_recv.at[d], {"gy": across})
+
+    def c_copy(d, slot):
+        part = gat.at[from_z(d), slot]
+        return remote(part, part, c_send.at[d], c_recv.at[d], {"gy": pair})
+
+    def f_copy(d, slot):
+        part = gat.at[from_z(d), slot]
+        return remote(part, part, f_send.at[d], f_recv.at[d], {"gy": pair})
+
+    for d in range(1, nz):
+        t_copy(d).start()
+    gat[z, j] = at[z]
+    for d in range(nz):
+        if d > 0:
+            t_arrival(d).wait_recv()
+        x_copy(d, j).start()
+        c_copy(d, j).start()
+    for d in range(nz):
+        x_copy(d, across).wait_recv()
+        f_copy(d, across).start()
+    for d in range(nz):
+        c_copy(d, pair).wait_recv()
+        f_copy(d, diag).wait_recv()
+        stacked = moved("rows", gat[from_z(d)].reshape(-1, hd))
+        for h in range(heads):
+            am[from_z(d), :, h * hd : (h + 1) * hd] = stacked[h * rows : (h + 1) * rows]
+    for k in range(kparts):
+        wo_in(k).wait()
+
+    def spot(n, d, which):
+        return (pl.ds(pl.multiple_of((n * nz + d) * rows, rows), rows), pl.ds(which * oc, oc))
+
+    def o_right(n, d):
+        return remote(
+            wq.at[spot(n, d, 2)], wq.at[spot(n, d, 0)], o_send.at[n, d], ol_recv.at[n, d], {"gx": lax.rem(z + 1, nz)}
+        )
+
+    def o_left(n, d):
+        return remote(
+            wq.at[spot(n, d, 2)], wq.at[spot(n, d, 1)], o_send.at[n, d], or_recv.at[n, d], {"gx": lax.rem(z + nz - 1, nz)}
+        )
+
+    @pl.loop(0, oparts)
+    def _(n):
+        cols = pl.ds(pl.multiple_of(n * oc, oc), oc)
+        part = jnp.dot(am[...].reshape(nz * rows, slice_width), wo[:, cols], preferred_element_type=jnp.float32)
+        po[:, :, cols] = part.reshape(nz, rows, oc)
+
+        @pl.when(z == 0)
+        def _():
+            for d in range(nz - 1, 0, -1):
+                wq[spot(n, d, 2)] = po[d, :, cols].astype(jnp.bfloat16)
+                o_right(n, d).start()
+
+        @pl.when(z == nz - 1)
+        def _():
+            for d in range(nz - 1):
+                wq[spot(n, d, 2)] = po[d, :, cols].astype(jnp.bfloat16)
+                o_left(n, d).start()
+
+    @pl.loop(0, oparts)
+    def _(n):
+        cols = pl.ds(pl.multiple_of(n * oc, oc), oc)
+        for d in range(nz - 1, 1, -1):
+            @pl.when((z > 0) & (z < d))
+            def _():
+                o_right(n, d).wait_recv()
+                wq[spot(n, d, 2)] = (po[d, :, cols] + wq[spot(n, d, 0)].astype(jnp.float32)).astype(jnp.bfloat16)
+                o_right(n, d).start()
+        for d in range(nz - 2):
+            @pl.when((z < nz - 1) & (z > d))
+            def _():
+                o_left(n, d).wait_recv()
+                wq[spot(n, d, 2)] = (po[d, :, cols] + wq[spot(n, d, 1)].astype(jnp.float32)).astype(jnp.bfloat16)
+                o_left(n, d).start()
+
+        @pl.when(z > 0)
+        def _():
+            o_right(n, z).wait_recv()
+            po[z, :, cols] += wq[spot(n, z, 0)].astype(jnp.float32)
+
+        @pl.when(z < nz - 1)
+        def _():
+            o_left(n, z).wait_recv()
+            po[z, :, cols] += wq[spot(n, z, 1)].astype(jnp.float32)
+
+        out_ref[:, cols] = po[z, :, cols].astype(jnp.bfloat16)
+
+    for t in range(nz):
+        for k in range(kparts):
+            @pl.when((z - t >= 0) & (z < nz - 1))
+            def _():
+                hid_right(z - t, k).wait_send()
+
+            @pl.when((z + t < nz) & (z > 0))
+            def _():
+                hid_left(z + t, k).wait_send()
+    for n in range(qparts):
+        stage_a(1, n).wait_send()
+        stage_a(0, n).wait_send()
+        stage_b(n).wait_send()
+    for d in range(nz):
+        if d > 0:
+            q_copy(d).wait_send()
+            t_copy(d).wait_send()
+        x_copy(d, j).wait_send()
+        c_copy(d, j).wait_send()
+        f_copy(d, across).wait_send()
+
+    @pl.loop(0, oparts)
+    def _(n):
+        for d in range(nz):
+            @pl.when(z < d)
+            def _():
+                o_right(n, d).wait_send()
+
+            @pl.when(z > d)
+            def _():
+                o_left(n, d).wait_send()
+
+
+def fused(hidden_in, w_query, w_out, cache_keys, cache_values, lengths):
+    nz, ny = lax.axis_size("gx"), lax.axis_size("gy")
+    rows = hidden_in.shape[0]
+    seqs, slots, hd = cache_keys.shape
+    depth, slice_width = w_query.shape
+    width = w_out.shape[1]
+    heads = slice_width // hd
+    block = seqs * heads
+    kparts, qparts, oparts = pieces(depth, 6), pieces(slice_width, 4), pieces(width, 6)
+    kparts = kparts if slice_width % (kparts * 16) == 0 else 1
+    parts = {
+        "in": permutation((nz, ny, seqs), (1, 0, 2)),
+        "query": permutation((heads, nz, seqs), (1, 2, 0)),
+        "heads": permutation((nz, seqs, heads), (1, 0, 2)),
+        "back": permutation((seqs, nz, heads), (1, 0, 2)),
+        "rows": permutation((ny, seqs, heads), (2, 0, 1)),
+    }
+    spots, start, widest = {}, 0, -(-max(m.shape[0] for m in parts.values()) // 128) * 128
+    packed = []
+    for name, m in parts.items():
+        spots[name] = (start, m.shape[0])
+        start += m.shape[0]
+        packed.append(np.pad(m, ((0, 0), (0, widest - m.shape[0]))))
+    perms = jnp.asarray(np.concatenate(packed, axis=0), jnp.bfloat16)
+    bf16, f32 = jnp.bfloat16, jnp.float32
+    dma = pltpu.SemaphoreType.DMA
+    anywhere = pl.BlockSpec(memory_space=pl.ANY)
+    return pl.pallas_call(
+        functools.partial(kernel, nz, seqs, heads, kparts, qparts, oparts, spots),
+        out_shape=jax.ShapeDtypeStruct((rows, width), bf16),
+        in_specs=[anywhere] * 6 + [pl.BlockSpec(memory_space=pltpu.SMEM)],
+        out_specs=pl.BlockSpec(memory_space=pltpu.VMEM),
+        scratch_shapes=[
+            pltpu.VMEM(w_query.shape, bf16),
+            pltpu.VMEM(w_out.shape, bf16),
+            pltpu.VMEM(cache_keys.shape, bf16),
+            pltpu.VMEM(cache_values.shape, bf16),
+            pltpu.VMEM(perms.shape, bf16),
+            pltpu.VMEM((nz, rows, depth), bf16),
+            pltpu.VMEM((nz * rows, slice_width), f32),
+            pltpu.VMEM((2, rows, slice_width), f32),
+            pltpu.VMEM((rows, slice_width), f32),
+            pltpu.VMEM((rows, slice_width), f32),
+            pltpu.VMEM((nz, block, hd), bf16),
+            pltpu.VMEM((nz, block, hd), bf16),
+            pltpu.VMEM((nz, block, hd), bf16),
+            pltpu.VMEM((nz, ny, block, hd), bf16),
+            pltpu.VMEM((nz, rows, slice_width), bf16),
+            pltpu.VMEM((nz, rows, width), f32),
+            dma((4,)), dma((kparts,)), dma((kparts,)),
+            dma((nz, kparts)), dma((nz, kparts)), dma((nz, kparts)),
+            dma((2, qparts)), dma((2, qparts)), dma((qparts,)), dma((qparts,)),
+            dma((nz,)), dma((nz,)), dma((nz,)), dma((nz,)),
+            dma((nz,)), dma((nz,)), dma((nz,)), dma((nz,)), dma((nz,)), dma((nz,)),
+            dma((oparts, nz)), dma((oparts, nz)), dma((oparts, nz)),
+        ],
+        compiler_params=pltpu.CompilerParams(
+            collective_id=0, has_side_effects=True, vmem_limit_bytes=VMEM_LIMIT
+        ),
+    )(hidden_in, w_query, w_out, cache_keys, cache_values, perms, lengths)
+
+
+def plain(hidden_in, w_query, w_out, cache_keys, cache_values, lengths):
     across = lax.axis_size("gx")
     within = lax.axis_size("gy")
     local_seqs = cache_keys.shape[0]
@@ -41,6 +450,24 @@
     return result.astype(jnp.bfloat16)
 
 
+def body(hidden_in, w_query, w_out, cache_keys, cache_values, lengths):
+    nz, ny = lax.axis_size("gx"), lax.axis_size("gy")
+    rows, (seqs, slots, hd) = hidden_in.shape[0], cache_keys.shape
+    depth, slice_width = w_query.shape
+    width = w_out.shape[1]
+    fits = ny == 4 and nz > 1 and slice_width % hd == 0 and hd % 256 == 0 and slots % 128 == 0
+    fits = fits and rows % 16 == 0 and depth % 256 == 0 and width % 256 == 0
+    if fits:
+        tokens, block = nz * rows, seqs * (slice_width // hd)
+        stored = 2 * (2 * slice_width * depth + 2 * cache_keys.size)
+        working = tokens * (2 * depth + 6 * slice_width + 4 * width) + 16 * rows * slice_width
+        fits = block % 16 == 0 and (nz * slice_width // hd) % 16 == 0
+        fits = fits and tokens * 6 <= depth and stored + working + 2**20 < VMEM_LIMIT
+        fits = fits and 3 * (width // pieces(width, 6)) <= slice_width
+    run = fused if fits else plain
+    return run(hidden_in, w_query, w_out, cache_keys, cache_values, lengths)
+
+
 def solution(mesh):
     placed = (
         P(("groups", "gx"), "gy"),

time: 137 us -> 98.9 us (0.72)
  Pallas kernels: 0 us -> 97.2 us
  blocking collectives: 52.2 us -> 0 us
  waiting for transfers between devices: 33.6 us -> 0 us
  matrix products: 28.2 us -> 0 us
  between operations: 13.5 us -> 0.01 us
  starting transfers between devices: 4.82 us -> 0 us
  other arithmetic: 2.03 us -> 0 us
    pallas_call x0 -> x1, Pallas kernels: none -> 97.2 us  [fused(): pl.pallas_call(functools.partial(kernel, nz, seqs, heads, kparts, qparts,...]
    dot_general x4 -> x0, matrix products: 28.2 us -> none  [the longest x1 12.8 us: body(): partial_out = jnp.dot(head_rows, w_out, preferred_element_type=jnp.float32)]
    reduce_scatter x1 -> x0, waiting for transfers between devices: 27.8 us -> none  [body(): lax.psum_scatter(partial_out, 'gx', scatter_dimension=0, tiled=True)]
    all_gather x2 -> x0, blocking collectives: 24.7 us -> none  [the longest x1 18.6 us: body(): lax.all_gather(hidden_in, 'gx', axis=0, tiled=True)]
    psum x1 -> x0, blocking collectives: 19.3 us -> none  [body(): summed = lax.psum(partial_query, 'gy')]
    all_to_all x1 -> x0, blocking collectives: 8.21 us -> none  [body(): lax.all_to_all(attended, 'gx', split_axis=1, concat_axis=0, tiled=True)]
    all_to_all x1 -> x0, waiting for transfers between devices: 5.75 us -> none  [body(): lax.all_to_all(query_rows, 'gx', split_axis=0, concat_axis=1, tiled=True)]
    all_to_all x1 -> x0, starting transfers between devices: 4.81 us -> none  [body(): lax.all_to_all(query_rows, 'gx', split_axis=0, concat_axis=1, tiled=True)]
  transfers between devices with their start and end apart: 2 -> 0, of which waited for: 2 -> 0; matrix products, arithmetic and copies ran while one was open for 0% -> 0% of each run, Pallas kernels for 0% -> 0%
where the time goes in v1:
time: 98.9 us; the launch traced here: 98.8 us
  Pallas kernels  97.2 us (98%)
  local copies, waits for them, and re-layouts  1.58 us (2%)
    pallas_call x1, Pallas kernels, fused(): pl.pallas_call(functools.partial(kernel, nz, seqs, heads, kparts, qparts,...  97.2 us

profile of v1, /device:TPU:0, one launch (start us, length us, event | category | flops | bytes accessed | tf_op | source)
XLA Modules:
  0.0 98.8 jit_solution(1119833497881991574)
XLA Ops:
  0.0 97.2 %shard_map.73 = bf16[16,4608]{1,0:T(8,128)(2,1)} custom-call(bf16[16,4608]{1,0:T(8,128)(2,1)} %hidden_ref.1, bf16[4608,3072]{1,0:T(8,128)(2,1)} %wq_ref.1, bf16[3072,4608]{1,0:T(8,128)(2,1)} %wo_ref.1, bf16[4,1024,256]{2,1,0:T(8,128)(2,1)} %keys_ref.1, bf16[4,1024,256]{2,1,0:T(8,128)(2,1)} %values_ref.1, bf16[832,256]{1,0:T(8,128)(2,1)} %constant.2.clone.perm_ref, ...), custom_call_target="tpu_custom_call" | custom-call | tf_op jit(solution)/shard_map/pallas_call | solution.py:381
  97.2 1.6 %copy.9 = bf16[16,4608]{1,0:T(8,128)(2,1)} copy(bf16[16,4608]{1,0:T(8,128)(2,1)} %shard_map.73) | data formatting | bytes 294912

commit v2 on v1

--- a/solution.py
+++ b/solution.py
@@ -69,14 +69,14 @@
         part = pl.ds(k * (slice_width // kparts), slice_width // kparts)
         return pltpu.make_async_copy(wo_ref.at[part], wo.at[part], wo_sem.at[k])
 
-    for k in range(kparts):
-        wq_in(k).start()
-
     barrier = pltpu.get_barrier_semaphore()
     for d in range(1, nz):
         pl.semaphore_signal(barrier, inc=1, device_id={"gx": lax.rem(z + d, nz)}, device_id_type=MESH)
     for peer in (pair, across):
         pl.semaphore_signal(barrier, inc=1, device_id={"gy": peer}, device_id_type=MESH)
+    hid_in.wait()
+    for k in range(kparts):
+        wq_in(k).start()
     pl.semaphore_wait(barrier, nz + 1)
 
     def hid_right(src, k):
@@ -87,8 +87,7 @@
         part = hid.at[src, :, pl.ds(k * kc, kc)]
         return remote(part, part, hl_sem.at[src, k], hid_sem.at[src, k], {"gx": lax.rem(z + nz - 1, nz)})
 
-    hid_in.wait()
-    for k in range(kparts):
+    def send_own(k):
         @pl.when(z < nz - 1)
         def _():
             hid_right(z, k).start()
@@ -97,7 +96,9 @@
         def _():
             hid_left(z, k).start()
 
-    perm_in.wait()
+    ahead = min(2, kparts)
+    for k in range(ahead):
+        send_own(k)
 
     def perm(name):
         start, size = spots[name]
@@ -112,52 +113,60 @@
         src = pq.at[pl.ds(pl.multiple_of((there * 2 + co) * rows, rows), rows), cols]
         return remote(src, r1.at[1 if far else 0, :, cols], a_send.at[far, n], a_recv.at[far, n], {"gy": pair})
 
-    for t in range(1, nz):
-        for k in range(kparts):
-            @pl.when(z - t >= 0)
-            def _():
-                hid_right(z - t, k).wait_recv()
-
-                @pl.when(z < nz - 1)
-                def _():
-                    hid_right(z - t, k).start()
-
-            @pl.when(z + t < nz)
-            def _():
-                hid_left(z + t, k).wait_recv()
-
-                @pl.when(z > 0)
-                def _():
-                    hid_left(z + t, k).start()
-
-            if t == max(nz - 2, 1):
-                wq_in(k).wait()
-                wo_in(k).start()
-                if k == 0:
-                    keys_in.start()
-                    values_in.start()
-            if t == nz - 1:
-                piece = hid[:, :, k * kc : (k + 1) * kc].reshape(nz * rows, kc)
-                piece = moved("in", piece)
-                depths = slice(k * kc, (k + 1) * kc)
-
-                if k < kparts - 1:
-                    @pl.loop(0, qparts)
-                    def _(n):
-                        cols = pl.ds(pl.multiple_of(n * qc, qc), qc)
-                        part = jnp.dot(piece, wq[depths, cols], preferred_element_type=jnp.float32)
-                        if k > 0:
-                            part = part + pq[:, cols]
-                        pq[:, cols] = part
-                else:
-                    for n in range(qparts):
-                        cols = slice(n * qc, (n + 1) * qc)
-                        part = jnp.dot(piece, wq[depths, cols], preferred_element_type=jnp.float32)
-                        if k > 0:
-                            part = part + pq[:, cols]
-                        pq[:, cols] = part
-                        stage_a(1, n).start()
-                        stage_a(0, n).start()
+    def pass_on(t, k):
+        @pl.when(z - t >= 0)
+        def _():
+            hid_right(z - t, k).wait_recv()
+
+            @pl.when(z < nz - 1)
+            def _():
+                hid_right(z - t, k).start()
+
+        @pl.when(z + t < nz)
+        def _():
+            hid_left(z + t, k).wait_recv()
+
+            @pl.when(z > 0)
+            def _():
+                hid_left(z + t, k).start()
+
+    for step in range(kparts + 2 * (nz - 1)):
+        if ahead <= step < kparts:
+            send_own(step)
+        for t in range(1, nz):
+            if 0 <= step - 2 * t < kparts:
+                pass_on(t, step - 2 * t)
+        if 2 <= step < kparts + 2:
+            wq_in(step - 2).wait()
+            wo_in(step - 2).start()
+        k = step - 2 * (nz - 1)
+        if k < 0:
+            continue
+        if k == 0:
+            keys_in.start()
+            values_in.start()
+            perm_in.wait()
+        piece = hid[:, :, k * kc : (k + 1) * kc].reshape(nz * rows, kc)
+        piece = moved("in", piece)
+        depths = slice(k * kc, (k + 1) * kc)
+
+        if k < kparts - 1:
+            @pl.loop(0, qparts)
+            def _(n):
+                cols = pl.ds(pl.multiple_of(n * qc, qc), qc)
+                part = jnp.dot(piece, wq[depths, cols], preferred_element_type=jnp.float32)
+                if k > 0:
+                    part = part + pq[:, cols]
+                pq[:, cols] = part
+        else:
+            for n in range(qparts):
+                cols = slice(n * qc, (n + 1) * qc)
+                part = jnp.dot(piece, wq[depths, cols], preferred_element_type=jnp.float32)
+                if k > 0:
+                    part = part + pq[:, cols]
+                pq[:, cols] = part
+                stage_a(1, n).start()
+                stage_a(0, n).start()
 
     def stage_b(n):
         cols = pl.ds(n * qc, qc)
@@ -260,7 +269,9 @@
         wo_in(k).wait()
 
     def spot(n, d, which):
-        return (pl.ds(pl.multiple_of((n * nz + d) * rows, rows), rows), pl.ds(which * oc, oc))
+        start = (n * nz + d) * rows
+        start = start if isinstance(start, int) else pl.multiple_of(start, rows)
+        return (pl.ds(start, rows), pl.ds(which * oc, oc))
 
     def o_right(n, d):
         return remote(
@@ -272,39 +283,67 @@
             wq.at[spot(n, d, 2)], wq.at[spot(n, d, 1)], o_send.at[n, d], or_recv.at[n, d], {"gx": lax.rem(z + nz - 1, nz)}
         )
 
-    @pl.loop(0, oparts)
-    def _(n):
-        cols = pl.ds(pl.multiple_of(n * oc, oc), oc)
-        part = jnp.dot(am[...].reshape(nz * rows, slice_width), wo[:, cols], preferred_element_type=jnp.float32)
-        po[:, :, cols] = part.reshape(nz, rows, oc)
-
-        @pl.when(z == 0)
-        def _():
-            for d in range(nz - 1, 0, -1):
-                wq[spot(n, d, 2)] = po[d, :, cols].astype(jnp.bfloat16)
-                o_right(n, d).start()
-
-        @pl.when(z == nz - 1)
-        def _():
-            for d in range(nz - 1):
-                wq[spot(n, d, 2)] = po[d, :, cols].astype(jnp.bfloat16)
-                o_left(n, d).start()
-
-    @pl.loop(0, oparts)
-    def _(n):
-        cols = pl.ds(pl.multiple_of(n * oc, oc), oc)
-        for d in range(nz - 1, 1, -1):
-            @pl.when((z > 0) & (z < d))
-            def _():
-                o_right(n, d).wait_recv()
-                wq[spot(n, d, 2)] = (po[d, :, cols] + wq[spot(n, d, 0)].astype(jnp.float32)).astype(jnp.bfloat16)
-                o_right(n, d).start()
-        for d in range(nz - 2):
-            @pl.when((z < nz - 1) & (z > d))
-            def _():
-                o_left(n, d).wait_recv()
-                wq[spot(n, d, 2)] = (po[d, :, cols] + wq[spot(n, d, 1)].astype(jnp.float32)).astype(jnp.bfloat16)
-                o_left(n, d).start()
+    def send_right(n, d):
+        cols = slice(n * oc, (n + 1) * oc)
+
+        @pl.when((z > 0) & (z < d))
+        def _():
+            o_right(n, d).wait_recv()
+            wq[spot(n, d, 2)] = (po[d, :, cols] + wq[spot(n, d, 0)].astype(jnp.float32)).astype(jnp.bfloat16)
+            o_right(n, d).start()
+
+    def send_left(n, d):
+        cols = slice(n * oc, (n + 1) * oc)
+
+        @pl.when((z < nz - 1) & (z > d))
+        def _():
+            o_left(n, d).wait_recv()
+            wq[spot(n, d, 2)] = (po[d, :, cols] + wq[spot(n, d, 1)].astype(jnp.float32)).astype(jnp.bfloat16)
+            o_left(n, d).start()
+
+    def relay(step, near):
+        for d in range(nz - 1, 0, -1):
+            n = step - (nz - 1 - d)
+            if 0 <= n < oparts:
+                @pl.when((2 * z < nz) if near else (2 * z >= nz))
+                def _():
+                    send_right(n, d)
+        for d in range(nz - 1):
+            n = step - d
+            if 0 <= n < oparts:
+                @pl.when((2 * z >= nz) if near else (2 * z < nz))
+                def _():
+                    send_left(n, d)
+
+    spent = oparts + nz - 2
+    for step in range(spent + 4):
+        if step < oparts:
+            cols = slice(step * oc, (step + 1) * oc)
+            part = jnp.dot(am[...].reshape(nz * rows, slice_width), wo[:, cols], preferred_element_type=jnp.float32)
+            po[:, :, cols] = part.reshape(nz, rows, oc)
+        if step < spent:
+            @pl.when(z == 0)
+            def _():
+                for d in range(nz - 1, 0, -1):
+                    n = step - (nz - 1 - d)
+                    if 0 <= n < oparts:
+                        wq[spot(n, d, 2)] = po[d, :, n * oc : (n + 1) * oc].astype(jnp.bfloat16)
+                        o_right(n, d).start()
+
+            @pl.when(z == nz - 1)
+            def _():
+                for d in range(nz - 1):
+                    n = step - d
+                    if 0 <= n < oparts:
+                        wq[spot(n, d, 2)] = po[d, :, n * oc : (n + 1) * oc].astype(jnp.bfloat16)
+                        o_left(n, d).start()
+        if step >= 2:
+            relay(step - 2, True)
+        if step >= 4:
+            relay(step - 4, False)
+
+    for n in range(oparts):
+        cols = slice(n * oc, (n + 1) * oc)
 
         @pl.when(z > 0)
         def _():

time: 98.9 us -> 65.4 us (0.66)
  Pallas kernels: 97.2 us -> 63.6 us
    pallas_call x1, Pallas kernels: 97.2 us -> 63.6 us  [fused(): pl.pallas_call(functools.partial(kernel, nz, seqs, heads, kparts, qparts,...]
where the time goes in v2:
time: 65.4 us; the launch traced here: 65.2 us
  Pallas kernels  63.6 us (97%)
  local copies, waits for them, and re-layouts  1.58 us (2%)
    pallas_call x1, Pallas kernels, fused(): pl.pallas_call(functools.partial(kernel, nz, seqs, heads, kparts, qparts,...  63.6 us
    unnamed x1, local copies, waits for them, and re-layouts  1.58 us

profile of v2, /device:TPU:0, one launch (start us, length us, event | category | flops | bytes accessed | tf_op | source)
XLA Modules:
  0.0 65.2 jit_solution(17418261235368585501)
XLA Ops:
  0.0 63.6 %shard_map.73 = bf16[16,4608]{1,0:T(8,128)(2,1)} custom-call(bf16[16,4608]{1,0:T(8,128)(2,1)} %hidden_ref.1, bf16[4608,3072]{1,0:T(8,128)(2,1)} %wq_ref.1, bf16[3072,4608]{1,0:T(8,128)(2,1)} %wo_ref.1, bf16[4,1024,256]{2,1,0:T(8,128)(2,1)} %keys_ref.1, bf16[4,1024,256]{2,1,0:T(8,128)(2,1)} %values_ref.1, bf16[832,256]{1,0:T(8,128)(2,1)} %constant.2.clone.perm_ref, ...), custom_call_target="tpu_custom_call" | custom-call | tf_op jit(solution)/shard_map/pallas_call | solution.py:420
  63.6 1.6 %copy.9 = bf16[16,4608]{1,0:T(8,128)(2,1)} copy(bf16[16,4608]{1,0:T(8,128)(2,1)} %shard_map.73) | data formatting | bytes 294912
